TPU v7x, 32 devices: a whole 2x2x4 slice. The times are simulated.
32 devices in a mesh: cuts: 8 (over y, x, core), mode: 4 (over z).
Axes of the slice: x: 2, y: 2, z: 4, core: 2. Of those that a mesh axis runs over, the one named last changes fastest.
Arguments:
- stem: float32 [8, 16, 16, 32768], P('cuts', 'mode'), may hold values from -1.5 to 1.5
- left: float32 [6, 2, 512, 512], P(None, None, 'mode'), may hold values from -0.25 to 0.25
- right: float32 [512, 512], replicated, may hold values from -0.25 to 0.25
- slice_bits: int32 [8, 6], P('cuts'), may hold values from 0 to 1
- leg_order: int32 [6, 9], replicated, may hold values from 0 to 8, each once within a row
Outputs:
- amplitudes: float32 [16, 16, 32768], P(None, 'mode', 'cuts')
Inputs may be any that keep to these rules, and one draw needn't show every extreme that they name: slice_bits[s, t] is the value of branch t's cut bond in slice s. Each row of leg_order is a permutation of 0 to 8.
All inputs are finite; a program needn't handle non-finite values.
Results may differ from a plain program's by a relative error of at most 0.00018.
Values sent between devices are 32-bit elements; how exact they have to be, the bound alone decides.
No kernel may reach another device: no remote copies, remote signals or barrier semaphores. Data moves between devices by JAX's collectives and lax.ppermute only.
A program may use at most 128 MiB of HBM per device.

v0:
```python
import jax
import jax.numpy as jnp
from jax import lax
from jax.sharding import PartitionSpec as P

HIGHEST_PRECISION = lax.Precision.HIGHEST


def leg_columns(leg_map, leg_count):
    indices = jnp.arange(2**leg_count, dtype=jnp.int32)
    shifts = leg_count - 1 - leg_map
    chosen = jnp.right_shift(indices[:, None], shifts[None, :]) & 1
    powers = jnp.left_shift(
        jnp.ones((leg_count,), jnp.int32), leg_count - 1 - jnp.arange(leg_count, dtype=jnp.int32)
    )
    return jnp.sum(chosen * powers[None, :], axis=1)


def per_device(stem, left, right, slice_bits, leg_order):
    slices, leading, middle, trailing = stem.shape
    leg_count = leg_order.shape[1]
    branch_size = 2**leg_count
    total_modes = 8 + trailing.bit_length() - 1
    devices_mode = lax.axis_size("mode")
    picked = jnp.where((slice_bits == 1)[:, :, None, None], left[None, :, 1], left[None, :, 0])

    def branch_right(branch):
        return jnp.take(right, leg_columns(leg_order[branch], leg_count), axis=1)

    def build(fragment, permuted):
        count_a, count_b, width = fragment.shape
        product = jnp.dot(
            fragment.reshape(count_a * count_b, width), permuted, precision=HIGHEST_PRECISION
        )
        return product.reshape(count_a, count_b, branch_size)

    def fetch(branch, kernel):
        return kernel(
            lax.all_gather(
                build(picked[:, branch], branch_right(branch)), "mode", axis=1, tiled=True
            ),
            jnp.int32(0),
        )

    def run_absorb(tensor, first, branch):
        after = 2 ** (total_modes - first - leg_count)
        prefix = tensor.shape[1] // (branch_size * after)
        if after == 1:
            shaped = tensor.reshape(slices, prefix, branch_size)

            def kernel(fragment, offset):
                return jnp.einsum("sji,spi->spj", fragment, shaped, precision=HIGHEST_PRECISION)

        else:
            shaped = tensor.reshape(slices, prefix, branch_size, after)

            def kernel(fragment, offset):
                return jnp.einsum("sji,spir->spjr", fragment, shaped, precision=HIGHEST_PRECISION)

        return fetch(branch, kernel).reshape(slices, -1)

    tensor = stem.reshape(slices, -1)
    tensor = run_absorb(tensor, total_modes - leg_count, 0)
    tensor = run_absorb(tensor, 6, 1)
    tensor = run_absorb(tensor, 4, 2)
    columns = middle // devices_mode
    head_states = leading * devices_mode
    inner_head = 2 ** (leg_count - 4)
    head_matrix = lax.all_gather(build(picked[:, 3], branch_right(3)), "mode", axis=1, tiled=True)
    head_blocks = head_matrix.reshape(slices, head_states, inner_head, head_states, inner_head)
    blocks = tensor.reshape(
        slices, leading, devices_mode, columns, inner_head, trailing // inner_head
    )
    received = lax.all_to_all(blocks, "mode", split_axis=2, concat_axis=1, tiled=True)
    arranged = received.reshape(slices, head_states, columns, inner_head, received.shape[5])
    result = jnp.einsum("sabcd,scxdr->saxbr", head_blocks, arranged, precision=HIGHEST_PRECISION)
    tensor = result.reshape(slices, -1)
    tensor = run_absorb(tensor, total_modes - leg_count, 4)
    inner_pair = 2 ** (leg_count - 2)
    shaped_pair = tensor.reshape(slices, 4, 4, columns, inner_pair, -1)

    def pair_kernel(fragment, offset):
        pieces = fragment.reshape(slices, fragment.shape[1], 4, inner_pair)
        return jnp.einsum("sjce,sacxer->sjaxr", pieces, shaped_pair, precision=HIGHEST_PRECISION)

    result = fetch(5, pair_kernel)
    result = result.reshape(slices, 4, inner_pair, 4, columns, -1).transpose(0, 3, 1, 4, 2, 5)
    tensor = result.reshape(slices, head_states, columns, trailing)
    summed = jnp.sum(tensor, axis=0)
    return lax.psum_scatter(summed, "cuts", scatter_dimension=2, tiled=True)


def solution(mesh):
    in_specs = (
        P("cuts", "mode", None, None),
        P(None, None, "mode", None),
        P(),
        P("cuts", None),
        P(),
    )
    out_specs = P(None, "mode", "cuts")
    return jax.shard_map(
        per_device, mesh=mesh, in_specs=in_specs, out_specs=out_specs, check_vma=False
    )
```

profile of v0, /device:TPU:0, one launch (start us, length us, event | category | flops | bytes accessed | tf_op | source)
XLA Modules:
  0.0 568.9 jit_solution(1955522628350760730)
XLA Ops:
  6.5 0.0 all-gather.15.cloned.1.call-start
  6.5 0.9 subtract_bitcast_fusion
  7.5 0.1 multiply_reduce_fusion.5
  7.6 1.6 copy.53
  9.2 0.7 compare_bitcast_fusion
  9.8 2.3 gather_fusion.1
  12.2 2.3 bitcast_select_fusion
  14.5 3.2 fusion.23
  17.7 0.0 all-gather.15.cloned.1.call-update
  17.7 0.0 all-gather.17.cloned.1.call-start
  17.8 2.3 gather_fusion.2
  20.1 3.2 fusion.21
  23.3 0.0 all-gather.17.cloned.1.call-update
  23.3 0.0 all-gather.19.cloned.1.call-start
  23.4 2.3 gather_fusion.3
  25.8 3.2 fusion.18
  29.0 0.0 all-gather.19.cloned.1.call-update
  29.0 9.4 %reshape.121 = f32[4096,512]{1,0:T(8,128)} reshape(f32[1,4,16,32768]{3,2,1,0:T(8,128)} %param.7) | data formatting | bytes 16777216 | tf_op jit(solution)/shard_map/reshape.2
  38.4 10.2 %all-gather.15.cloned.1.call-done = f32[512,512]{1,0:T(8,128)} async-done(((f32[128,512]{1,0:T(8,128)}), f32[512,512]{1,0:T(8,128)}) %all-gather.15.cloned.1.call-update) | async-done | bytes 1048592 | tf_op jit(solution)/shard_map/all_gather | solution.py:39
  48.6 17.5 %convolution_bitcast_fusion = f32[4096,512]{0,1:T(8,128)} fusion(f32[512,512]{1,0:T(8,128)} %all-gather.15.cloned.1.call-done, f32[4096,512]{1,0:T(8,128)} %reshape.121), kind=kOutput, calls=%fused_computation.9 | convolution fusion | flops 12884901888 | bytes 17825792 | tf_op jit(solution)/shard_map/sji,spi->spj/dot_general | solution.py:52
  66.0 9.0 %copy.55 = f32[4096,512]{1,0:T(8,128)} copy(f32[4096,512]{0,1:T(8,128)} %convolution_bitcast_fusion) | data formatting | bytes 16777216 | tf_op jit(solution)/shard_map/sji,spi->spj/dot_general | solution.py:52
  75.0 9.4 %reshape.122 = f32[16,512,256]{2,1,0:T(8,128)} reshape(f32[4096,512]{1,0:T(8,128)} %copy.55) | data formatting | bytes 16777216 | tf_op jit(solution)/shard_map/reshape.6
  84.4 0.0 all-gather.17.cloned.1.call-done
  84.4 30.5 %convolution_bitcast_fusion.1 = f32[1,16,512,256]{2,3,1,0:T(8,128)} fusion(f32[16,512,256]{2,1,0:T(8,128)} %reshape.122, f32[512,512]{1,0:T(8,128)} %all-gather.17.cloned.1.call-done), kind=kOutput, calls=%fused_computation.14 | convolution fusion | flops 12884901888 | bytes 17825792 | tf_op jit(solution)/shard_map/sji,spir->spjr/dot_general | solution.py:58
  114.9 9.3 %copy.58 = f32[1,16,512,256]{3,2,1,0:T(8,128)} copy(f32[1,16,512,256]{2,3,1,0:T(8,128)} %convolution_bitcast_fusion.1) | data formatting | bytes 16777216 | tf_op jit(solution)/shard_map/sji,spir->spjr/transpose | solution.py:58
  124.2 9.7 %reshape.125 = f32[4,512,1024]{2,1,0:T(8,128)} reshape(f32[1,16,512,256]{3,2,1,0:T(8,128)} %copy.58) | data formatting | bytes 16777216 | tf_op jit(solution)/shard_map/reshape.9
  133.9 0.0 all-gather.19.cloned.1.call-done
  133.9 18.2 %fusion.16 = f32[4,1024,512]{1,2,0:T(8,128)S(1)} fusion(f32[4,512,1024]{2,1,0:T(8,128)} %reshape.125, f32[512,512]{1,0:T(8,128)} %all-gather.19.cloned.1.call-done), kind=kOutput, calls=%fused_computation.21 | convolution fusion | flops 12884901888 | bytes 17825792 | tf_op jit(solution)/shard_map/sji,spir->spjr/dot_general | solution.py:58
  152.2 4.1 copy.60
  156.2 5.6 all-to-all-start
  161.9 0.0 all-gather.21.cloned.1.call-start
  161.9 2.5 gather_fusion.4
  164.5 3.2 fusion.14
  167.7 0.0 all-gather.21.cloned.1.call-update
  167.7 0.0 all-gather.13.cloned.1.call-start
  167.8 2.3 gather_fusion
  170.1 3.2 fusion.26
  173.3 0.0 all-gather.13.cloned.1.call-update
  173.3 0.0 all-gather.23.cloned.1.call-start
  173.4 2.3 gather_fusion.5
  175.7 3.2 fusion.12
  179.0 0.0 all-gather.23.cloned.1.call-update
  179.0 0.0 reduce-scatter.2.cloned.1.call-start
  179.1 57.4 %all-gather.21.cloned.1.call-done = f32[512,512]{1,0:T(8,128)} async-done(((f32[128,512]{1,0:T(8,128)}), f32[512,512]{1,0:T(8,128)}) %all-gather.21.cloned.1.call-update) | async-done | bytes 1048592 | tf_op jit(solution)/shard_map/all_gather | solution.py:69
  236.5 3.8 reshape.130
  240.2 37.6 %all-gather.13.cloned.1.call-done = f32[512,512]{1,0:T(8,128)} async-done(((f32[128,512]{1,0:T(8,128)}), f32[512,512]{1,0:T(8,128)}) %all-gather.13.cloned.1.call-update) | async-done | bytes 1048592 | tf_op jit(solution)/shard_map/all_gather | solution.py:39
  277.9 1.6 reshape.118
  279.5 115.9 %all-to-all-done = f32[1,4,4,4,32,1024]{5,4,3,1,0,2:T(8,128)} async-done(((f32[1,4,4,4,32,1024]{5,4,3,1,0,2:T(8,128)}), f32[1,4,4,4,32,1024]{5,4,3,1,0,2:T(8,128)}, u32[]{:S(2)}, u32[]{:S(2)}) %all-to-all-start) | async-done | bytes 8388640 | tf_op jit(solution)/shard_map/all_to_all | solution.py:74
  395.4 0.0 copy-start
  395.4 4.4 copy.61
  399.8 0.2 copy-done
  399.9 18.9 %fusion.9 = f32[1,16,4,32,1024]{4,3,1,2,0:T(8,128)S(1)} fusion(f32[16,4,32,1024,1]{3,2,0,4,1:T(8,128)S(1)} %bitcast.122, f32[16,32,16,32]{3,2,1,0:T(8,128)S(1)} %copy-done), kind=kOutput, calls=%fused_computation.15 | convolution fusion | flops 12884901888 | bytes 17825792 | tf_op jit(solution)/shard_map/sabcd,scxdr->saxbr/dot_general | solution.py:76
  418.9 4.1 copy.64
  422.9 9.4 %reshape.131 = f32[4096,512]{1,0:T(8,128)} reshape(f32[1,16,4,32,1024]{4,3,2,1,0:T(8,128)} %copy.64) | data formatting | bytes 16777216 | tf_op jit(solution)/shard_map/reshape.27
  432.3 0.0 all-gather.23.cloned.1.call-done
  432.3 17.7 %fusion.52 = f32[4096,512]{1,0:T(8,128)} fusion(f32[4096,512]{1,0:T(8,128)} %reshape.131, f32[512,512]{1,0:T(8,128)} %all-gather.23.cloned.1.call-done), kind=kOutput, calls=%fused_computation.95 | convolution fusion | flops 12884901888 | bytes 17825792 | tf_op jit(solution)/shard_map/sji,spi->spj/dot_general | solution.py:52
  450.0 9.4 %reshape.134 = f32[4,4,4,128,256]{4,3,2,1,0:T(8,128)} reshape(f32[4096,512]{1,0:T(8,128)} %fusion.52) | data formatting | bytes 16777216 | tf_op jit(solution)/shard_map/reshape.32
  459.3 16.0 %fusion.6 = f32[1,4,4,4,128,256]{5,4,3,1,2,0:T(8,128)S(1)} fusion(f32[4,4,4,128,256]{4,3,2,1,0:T(8,128)} %reshape.134, f32[4,128,4,128,1,1]{3,2,1,0,5,4:T(4,128)S(1)} %bitcast.123), kind=kOutput, calls=%fused_computation.13 | convolution fusion | flops 12884901888 | bytes 17825792 | tf_op jit(solution)/shard_map/sjce,sacxer->sjaxr/dot_general | solution.py:84
  475.3 3.8 copy.68
  479.1 9.4 %reduce_sum.66 = f32[16,4,32768]{2,0,1:T(8,128)} reshape(f32[1,4,4,4,128,256]{5,4,2,1,3,0:T(8,128)} %copy.68) | data formatting | bytes 16777216 | tf_op jit(solution)/shard_map/reduce_sum | solution.py:89
  488.5 0.0 reduce-scatter.2.cloned.1.call-update
  488.5 70.5 %reduce-scatter.2.cloned.1.call-done = f32[16,4,4096]{2,0,1:T(8,128)} async-done(((f32[16,4,32768]{2,0,1:T(8,128)}), f32[16,4,4096]{2,0,1:T(8,128)}) %reduce-scatter.2.cloned.1.call-update) | async-done | bytes 1048592 | tf_op jit(solution)/shard_map/reduce_scatter | solution.py:90
  559.0 2.9 copy.69
  (19 shorter events, 0.1 us)
Async XLA Ops:
  6.5 42.0 %all-gather.15.cloned.1.call-start = ((), (), s32[]{:S(2)}) async-start(), calls=%async_computation.4 | async-start | bytes 1310720 | tf_op jit(solution)/shard_map/all_gather | solution.py:39
  17.7 66.7 %all-gather.17.cloned.1.call-start = ((), (), s32[]{:S(2)}) async-start(), calls=%async_computation.5 | async-start | bytes 1310720 | tf_op jit(solution)/shard_map/all_gather | solution.py:39
  23.3 110.6 %all-gather.19.cloned.1.call-start = ((), (), s32[]{:S(2)}) async-start(), calls=%async_computation.6 | async-start | bytes 1310720 | tf_op jit(solution)/shard_map/all_gather | solution.py:39
  156.2 239.1 %all-to-all-start = ((f32[1,4,4,4,32,1024]{5,4,3,1,0,2:T(8,128)}), f32[1,4,4,4,32,1024]{5,4,3,1,0,2:T(8,128)}, u32[]{:S(2)}, u32[]{:S(2)}) async-start(f32[1,4,4,4,32,1024]{5,4,3,1,0,2:T(8,128)} %copy.60), calls=%async_computation | async-start | bytes 16777216 | tf_op jit(solution)/shard_map/all_to_all | solution.py:74
  161.9 74.6 %all-gather.21.cloned.1.call-start = ((), (), s32[]{:S(2)}) async-start(), calls=%async_computation.7 | async-start | bytes 1310720 | tf_op jit(solution)/shard_map/all_gather | solution.py:69
  167.7 110.2 %all-gather.13.cloned.1.call-start = ((), (), s32[]{:S(2)}) async-start(), calls=%async_computation.3 | async-start | bytes 1310720 | tf_op jit(solution)/shard_map/all_gather | solution.py:39
  173.3 259.0 %all-gather.23.cloned.1.call-start = ((), (), s32[]{:S(2)}) async-start(), calls=%async_computation.8 | async-start | bytes 1310720 | tf_op jit(solution)/shard_map/all_gather | solution.py:39
  179.0 380.0 %reduce-scatter.2.cloned.1.call-start = ((), (), s32[]{:S(2)}) async-start(), calls=%async_computation.2 | async-start | bytes 9437184 | tf_op jit(solution)/shard_map/reduce_scatter | solution.py:90
  395.4 4.6 copy-start
Sparse Core Ops, SparseCore 0:
  17.8 30.7 all-gather.14
  50.1 27.3 all-gather.16
  79.1 27.3 all-gather.18
  167.8 68.6 all-gather.20
  237.9 39.9 all-gather.12
  279.3 100.0 all-gather.22
  488.6 70.3 reduce-scatter.1
where the time goes:
time: 578 us; the launch traced here: 569 us
  waiting for transfers between devices  292 us (51%)
  matrix products  138 us (24%)
  local copies, waits for them, and re-layouts  115 us (20%)
  between operations  13.9 us (2%)
  starting transfers between devices  5.9 us (1%)
    all_to_all x1, waiting for transfers between devices, per_device(): lax.all_to_all(blocks, 'mode', split_axis=2, concat_axis=1, tiled=True)  116 us
    reduce_scatter x1, waiting for transfers between devices, per_device(): return lax.psum_scatter(summed, 'cuts', scatter_dimension=2, tiled=True)  70.5 us
    all_gather x1, waiting for transfers between devices, per_device(): lax.all_gather(build(picked[:, 3], branch_right(3)), 'mode', axis=1, tile...  57.4 us
    another operation x7, local copies, waits for them, and re-layouts  52.6 us
    dot_general x2, matrix products, kernel(): jnp.einsum('sji,spir->spjr', fragment, shaped, precision=HIGHEST_PRECISION)  48.7 us
    all_gather x5, waiting for transfers between devices, fetch(): lax.all_gather(build(picked[:, branch], branch_right(branch)), 'mode', ax...  47.8 us
    dot_general x2, matrix products, kernel(): jnp.einsum('sji,spi->spj', fragment, shaped, precision=HIGHEST_PRECISION)  35.1 us
    dot_general x6, matrix products, build(): jnp.dot(fragment.reshape(count_a * count_b, width), permuted, precision=H...  19.3 us
  transfers between devices with their start and end apart: 8, of which 5 were waited for; matrix products, arithmetic and copies ran while one was open for 29% of the time, Pallas kernels for 0%

commit v1 on v0

--- a/solution.py
+++ b/solution.py
@@ -71,7 +71,10 @@
     blocks = tensor.reshape(
         slices, leading, devices_mode, columns, inner_head, trailing // inner_head
     )
-    received = lax.all_to_all(blocks, "mode", split_axis=2, concat_axis=1, tiled=True)
+    received = jnp.concatenate(
+        lax.all_to_all(jnp.stack(jnp.split(blocks, lax.axis_size("mode"), axis=2)), "mode", 0, 0),
+        axis=1,
+    )
     arranged = received.reshape(slices, head_states, columns, inner_head, received.shape[5])
     result = jnp.einsum("sabcd,scxdr->saxbr", head_blocks, arranged, precision=HIGHEST_PRECISION)
     tensor = result.reshape(slices, -1)

time: 578 us -> 579 us (level)
  no operation moved by 1% of the time
where the time goes in v1:
time: 579 us; the launch traced here: 570 us
  waiting for transfers between devices  292 us (50%)
  matrix products  138 us (24%)
  local copies, waits for them, and re-layouts  113 us (20%)
  between operations  13.9 us (2%)
  other arithmetic  7.64 us (1%)
  starting transfers between devices  5.91 us (1%)
    all_to_all x1, waiting for transfers between devices, per_device(): lax.all_to_all(jnp.stack(jnp.split(blocks, lax.axis_size('mode'), axis=2)...  116 us
    reduce_scatter x1, waiting for transfers between devices, per_device(): return lax.psum_scatter(summed, 'cuts', scatter_dimension=2, tiled=True)  70.5 us
    all_gather x1, waiting for transfers between devices, per_device(): lax.all_gather(build(picked[:, 3], branch_right(3)), 'mode', axis=1, tile...  57.4 us
    another operation x7, local copies, waits for them, and re-layouts  52.6 us
    dot_general x2, matrix products, kernel(): jnp.einsum('sji,spir->spjr', fragment, shaped, precision=HIGHEST_PRECISION)  48.8 us
    all_gather x5, waiting for transfers between devices, fetch(): lax.all_gather(build(picked[:, branch], branch_right(branch)), 'mode', ax...  47.8 us
    dot_general x2, matrix products, kernel(): jnp.einsum('sji,spi->spj', fragment, shaped, precision=HIGHEST_PRECISION)  35.2 us
    dot_general x6, matrix products, build(): jnp.dot(fragment.reshape(count_a * count_b, width), permuted, precision=H...  19.3 us
  transfers between devices with their start and end apart: 8, of which 5 were waited for; matrix products, arithmetic and copies ran while one was open for 29% of the time, Pallas kernels for 0%

profile of v1, /device:TPU:0, one launch (start us, length us, event | category | flops | bytes accessed | tf_op | source)
XLA Modules:
  0.0 570.2 jit_solution(503923572784328235)
XLA Ops:
  6.5 0.0 all-gather.15.cloned.1.call-start
  6.5 0.9 subtract_bitcast_fusion
  7.5 0.1 multiply_reduce_fusion.5
  7.6 1.6 copy.41
  9.2 0.7 compare_bitcast_fusion
  9.8 2.3 gather_fusion.1
  12.2 2.3 bitcast_select_fusion
  14.5 3.2 fusion.23
  17.7 0.0 all-gather.15.cloned.1.call-update
  17.7 0.0 all-gather.17.cloned.1.call-start
  17.8 2.3 gather_fusion.2
  20.1 3.2 fusion.21
  23.3 0.0 all-gather.17.cloned.1.call-update
  23.4 0.0 all-gather.19.cloned.1.call-start
  23.4 2.3 gather_fusion.3
  25.8 3.2 fusion.18
  29.0 0.0 all-gather.19.cloned.1.call-update
  29.0 9.4 %reshape.119 = f32[4096,512]{1,0:T(8,128)} reshape(f32[1,4,16,32768]{3,2,1,0:T(8,128)} %param.7) | data formatting | bytes 16777216 | tf_op jit(solution)/shard_map/reshape.2
  38.4 10.2 %all-gather.15.cloned.1.call-done = f32[512,512]{1,0:T(8,128)} async-done(((f32[128,512]{1,0:T(8,128)}), f32[512,512]{1,0:T(8,128)}) %all-gather.15.cloned.1.call-update) | async-done | bytes 1048592 | tf_op jit(solution)/shard_map/all_gather | solution.py:39
  48.6 17.5 %convolution_bitcast_fusion = f32[4096,512]{0,1:T(8,128)} fusion(f32[512,512]{1,0:T(8,128)} %all-gather.15.cloned.1.call-done, f32[4096,512]{1,0:T(8,128)} %reshape.119), kind=kOutput, calls=%fused_computation.10 | convolution fusion | flops 12884901888 | bytes 17825792 | tf_op jit(solution)/shard_map/sji,spi->spj/dot_general | solution.py:52
  66.1 9.0 %copy.43 = f32[4096,512]{1,0:T(8,128)} copy(f32[4096,512]{0,1:T(8,128)} %convolution_bitcast_fusion) | data formatting | bytes 16777216 | tf_op jit(solution)/shard_map/sji,spi->spj/dot_general | solution.py:52
  75.1 9.4 %reshape.120 = f32[16,512,256]{2,1,0:T(8,128)} reshape(f32[4096,512]{1,0:T(8,128)} %copy.43) | data formatting | bytes 16777216 | tf_op jit(solution)/shard_map/reshape.6
  84.5 0.0 all-gather.17.cloned.1.call-done
  84.5 30.5 %convolution_bitcast_fusion.1 = f32[1,16,512,256]{2,3,1,0:T(8,128)} fusion(f32[16,512,256]{2,1,0:T(8,128)} %reshape.120, f32[512,512]{1,0:T(8,128)} %all-gather.17.cloned.1.call-done), kind=kOutput, calls=%fused_computation.15 | convolution fusion | flops 12884901888 | bytes 17825792 | tf_op jit(solution)/shard_map/sji,spir->spjr/dot_general | solution.py:58
  115.0 9.3 %copy.46 = f32[1,16,512,256]{3,2,1,0:T(8,128)} copy(f32[1,16,512,256]{2,3,1,0:T(8,128)} %convolution_bitcast_fusion.1) | data formatting | bytes 16777216 | tf_op jit(solution)/shard_map/sji,spir->spjr/transpose | solution.py:58
  124.3 9.8 %reshape.123 = f32[4,512,1024]{2,1,0:T(8,128)} reshape(f32[1,16,512,256]{3,2,1,0:T(8,128)} %copy.46) | data formatting | bytes 16777216 | tf_op jit(solution)/shard_map/reshape.9
  134.0 0.0 all-gather.19.cloned.1.call-done
  134.0 18.2 %fusion.16 = f32[4,1024,512]{1,2,0:T(8,128)S(1)} fusion(f32[4,512,1024]{2,1,0:T(8,128)} %reshape.123, f32[512,512]{1,0:T(8,128)} %all-gather.19.cloned.1.call-done), kind=kOutput, calls=%fused_computation.26 | convolution fusion | flops 12884901888 | bytes 17825792 | tf_op jit(solution)/shard_map/sji,spir->spjr/dot_general | solution.py:58
  152.3 1.7 slice_bitcast_fusion.3
  153.9 3.5 pad_maximum_fusion
  157.5 5.7 all-to-all-start
  163.1 0.0 all-gather.21.cloned.1.call-start
  163.2 2.5 gather_fusion.4
  165.7 3.2 fusion.14
  168.9 0.0 all-gather.21.cloned.1.call-update
  169.0 0.0 all-gather.13.cloned.1.call-start
  169.0 2.3 gather_fusion
  171.4 3.2 fusion.26
  174.6 0.0 all-gather.13.cloned.1.call-update
  174.6 0.0 all-gather.23.cloned.1.call-start
  174.7 2.3 gather_fusion.5
  177.0 3.3 fusion.12
  180.2 0.0 all-gather.23.cloned.1.call-update
  180.3 0.0 reduce-scatter.2.cloned.1.call-start
  180.3 57.4 %all-gather.21.cloned.1.call-done = f32[512,512]{1,0:T(8,128)} async-done(((f32[128,512]{1,0:T(8,128)}), f32[512,512]{1,0:T(8,128)}) %all-gather.21.cloned.1.call-update) | async-done | bytes 1048592 | tf_op jit(solution)/shard_map/all_gather | solution.py:69
  237.7 3.8 reshape.128
  241.5 37.6 %all-gather.13.cloned.1.call-done = f32[512,512]{1,0:T(8,128)} async-done(((f32[128,512]{1,0:T(8,128)}), f32[512,512]{1,0:T(8,128)}) %all-gather.13.cloned.1.call-update) | async-done | bytes 1048592 | tf_op jit(solution)/shard_map/all_gather | solution.py:39
  279.2 1.6 reshape.116
  280.8 115.9 %all-to-all-done = f32[4,1,4,1,4,32,1024]{6,5,4,2,3,1,0:T(8,128)} async-done(((f32[4,1,4,1,4,32,1024]{6,5,4,2,3,1,0:T(8,128)}), f32[4,1,4,1,4,32,1024]{6,5,4,2,3,1,0:T(8,128)}, u32[]{:S(2)}, u32[]{:S(2)}) %all-to-all-start) | async-done | bytes 8388640 | tf_op jit(solution)/shard_map/all_to_all | solution.py:75
  396.6 0.0 copy-start
  396.6 4.4 copy.51
  401.0 0.2 copy-done
  401.2 18.9 %fusion.9 = f32[1,16,4,32,1024]{4,3,1,2,0:T(8,128)S(1)} fusion(f32[16,4,32,1024,1]{3,2,0,4,1:T(8,128)S(1)} %bitcast.133, f32[16,32,16,32]{3,2,1,0:T(8,128)S(1)} %copy-done), kind=kOutput, calls=%fused_computation.16 | convolution fusion | flops 12884901888 | bytes 17825792 | tf_op jit(solution)/shard_map/sabcd,scxdr->saxbr/dot_general | solution.py:79
  420.2 4.1 copy.54
  424.2 9.4 %reshape.129 = f32[4096,512]{1,0:T(8,128)} reshape(f32[1,16,4,32,1024]{4,3,2,1,0:T(8,128)} %copy.54) | data formatting | bytes 16777216 | tf_op jit(solution)/shard_map/reshape.25
  433.6 0.0 all-gather.23.cloned.1.call-done
  433.6 17.7 %fusion.52 = f32[4096,512]{1,0:T(8,128)} fusion(f32[4096,512]{1,0:T(8,128)} %reshape.129, f32[512,512]{1,0:T(8,128)} %all-gather.23.cloned.1.call-done), kind=kOutput, calls=%fused_computation.100 | convolution fusion | flops 12884901888 | bytes 17825792 | tf_op jit(solution)/shard_map/sji,spi->spj/dot_general | solution.py:52
  451.2 9.4 %reshape.132 = f32[4,4,4,128,256]{4,3,2,1,0:T(8,128)} reshape(f32[4096,512]{1,0:T(8,128)} %fusion.52) | data formatting | bytes 16777216 | tf_op jit(solution)/shard_map/reshape.30
  460.6 16.0 %fusion.6 = f32[1,4,4,4,128,256]{5,4,3,1,2,0:T(8,128)S(1)} fusion(f32[4,4,4,128,256]{4,3,2,1,0:T(8,128)} %reshape.132, f32[4,128,4,128,1,1]{3,2,1,0,5,4:T(4,128)S(1)} %bitcast.134), kind=kOutput, calls=%fused_computation.14 | convolution fusion | flops 12884901888 | bytes 17825792 | tf_op jit(solution)/shard_map/sjce,sacxer->sjaxr/dot_general | solution.py:87
  476.6 3.8 copy.58
  480.3 9.4 %reduce_sum.66 = f32[16,4,32768]{2,0,1:T(8,128)} reshape(f32[1,4,4,4,128,256]{5,4,2,1,3,0:T(8,128)} %copy.58) | data formatting | bytes 16777216 | tf_op jit(solution)/shard_map/reduce_sum | solution.py:92
  489.7 0.0 reduce-scatter.2.cloned.1.call-update
  489.8 70.5 %reduce-scatter.2.cloned.1.call-done = f32[16,4,4096]{2,0,1:T(8,128)} async-done(((f32[16,4,32768]{2,0,1:T(8,128)}), f32[16,4,4096]{2,0,1:T(8,128)}) %reduce-scatter.2.cloned.1.call-update) | async-done | bytes 1048592 | tf_op jit(solution)/shard_map/reduce_scatter | solution.py:93
  560.2 2.9 copy.59
  (19 shorter events, 0.1 us)
Async XLA Ops:
  6.5 42.0 %all-gather.15.cloned.1.call-start = ((), (), s32[]{:S(2)}) async-start(), calls=%async_computation.4 | async-start | bytes 1310720 | tf_op jit(solution)/shard_map/all_gather | solution.py:39
  17.7 66.8 %all-gather.17.cloned.1.call-start = ((), (), s32[]{:S(2)}) async-start(), calls=%async_computation.5 | async-start | bytes 1310720 | tf_op jit(solution)/shard_map/all_gather | solution.py:39
  23.4 110.7 %all-gather.19.cloned.1.call-start = ((), (), s32[]{:S(2)}) async-start(), calls=%async_computation.6 | async-start | bytes 1310720 | tf_op jit(solution)/shard_map/all_gather | solution.py:39
  157.5 239.2 %all-to-all-start = ((f32[4,1,4,1,4,32,1024]{6,5,4,2,3,1,0:T(8,128)}), f32[4,1,4,1,4,32,1024]{6,5,4,2,3,1,0:T(8,128)}, u32[]{:S(2)}, u32[]{:S(2)}) async-start(f32[4,1,4,1,4,32,1024]{6,5,4,2,3,1,0:T(8,128)} %pad_maximum_fusion), calls=%async_computation | async-start | bytes 16777216 | tf_op jit(solution)/shard_map/all_to_all | solution.py:75
  163.1 74.6 %all-gather.21.cloned.1.call-start = ((), (), s32[]{:S(2)}) async-start(), calls=%async_computation.7 | async-start | bytes 1310720 | tf_op jit(solution)/shard_map/all_gather | solution.py:69
  169.0 110.2 %all-gather.13.cloned.1.call-start = ((), (), s32[]{:S(2)}) async-start(), calls=%async_computation.3 | async-start | bytes 1310720 | tf_op jit(solution)/shard_map/all_gather | solution.py:39
  174.6 259.0 %all-gather.23.cloned.1.call-start = ((), (), s32[]{:S(2)}) async-start(), calls=%async_computation.8 | async-start | bytes 1310720 | tf_op jit(solution)/shard_map/all_gather | solution.py:39
  180.3 380.0 %reduce-scatter.2.cloned.1.call-start = ((), (), s32[]{:S(2)}) async-start(), calls=%async_computation.2 | async-start | bytes 9437184 | tf_op jit(solution)/shard_map/reduce_scatter | solution.py:93
  396.6 4.6 copy-start
Sparse Core Ops, SparseCore 0:
  17.8 30.7 all-gather.14
  50.1 27.3 all-gather.16
  79.1 27.3 all-gather.18
  169.1 68.6 all-gather.20
  239.1 39.9 all-gather.12
  280.6 100.0 all-gather.22
  489.9 70.3 reduce-scatter.1
